TPU v7x, 8 devices: a whole 2x2x1 slice. The times are simulated.
8 devices in a mesh: dp: 1 (over z), fsdp: 2 (over y), ep: 4 (over x, core).
Axes of the slice: x: 2, y: 2, z: 1, core: 2. Of those that a mesh axis runs over, the one named last changes fastest.
Arguments:
- hidden: bfloat16 [32768, 1024], P(('dp', 'fsdp', 'ep'))
- norm_gain: bfloat16 [1024], replicated
- w_router: bfloat16 [1024, 32], replicated
- w_gate: bfloat16 [32, 1024, 2816], P('ep', 'fsdp')
- w_up: bfloat16 [32, 1024, 2816], P('ep', 'fsdp')
- w_down: bfloat16 [32, 2816, 1024], P('ep', None, 'fsdp')
- top2_ids: int32 [32768, 2], P(('dp', 'fsdp', 'ep'))
Outputs:
- output: bfloat16 [32768, 1024], P(('dp', 'fsdp', 'ep'))
All inputs are finite; a program needn't handle non-finite values.
Results may differ from a plain program's by a relative error of at most 0.001.
Values are sent between devices in bfloat16 or wider.
A program may use at most 1 GiB of HBM per device.

v0:
```python
import jax
import jax.numpy as jnp
from jax import lax
from jax.sharding import PartitionSpec as P

EPS = 1e-5


def norm_and_gates(hidden, norm_gain, w_router, top2_ids):
    hidden_f32 = hidden.astype(jnp.float32)
    mean_sq = jnp.mean(hidden_f32 * hidden_f32, axis=-1, keepdims=True)
    normed = (hidden_f32 * lax.rsqrt(mean_sq + EPS) * norm_gain.astype(jnp.float32)).astype(jnp.bfloat16)
    logits = jnp.dot(normed, w_router, preferred_element_type=jnp.float32)
    gate_probs = jax.nn.softmax(jnp.take_along_axis(logits, top2_ids, axis=1), axis=-1)
    return hidden_f32, normed, gate_probs


def route_slots(top2_ids, num_experts, capacity):
    flat_ids = top2_ids.reshape(-1)
    onehot = (flat_ids[:, None] == jnp.arange(num_experts, dtype=jnp.int32)[None, :]).astype(jnp.int32)
    position = jnp.sum((jnp.cumsum(onehot, axis=0) - 1) * onehot, axis=1)
    slot_ids = jnp.where(position < capacity, flat_ids * capacity + position, num_experts * capacity)
    return slot_ids.reshape(top2_ids.shape)


def gather_rows(normed, slot_ids, num_slots):
    tok_count = slot_ids.shape[0]
    token_index = jnp.broadcast_to(jnp.arange(tok_count, dtype=jnp.int32)[:, None], slot_ids.shape)
    source = jnp.full((num_slots,), tok_count, dtype=jnp.int32).at[slot_ids.reshape(-1)].set(token_index.reshape(-1), mode='drop')
    return jnp.take(normed, source, axis=0, mode='fill', fill_value=0)


def take_slots(expert_rows, slot_ids):
    return jnp.take(expert_rows, slot_ids, axis=0, mode='fill', fill_value=0)


def expert_block(rows_in, gate_full, up_full, down_full):
    act_a = jnp.einsum('ecd,edf->ecf', rows_in, gate_full, preferred_element_type=jnp.float32)
    act_b = jnp.einsum('ecd,edf->ecf', rows_in, up_full, preferred_element_type=jnp.float32)
    hidden_act = (jax.nn.silu(act_a) * act_b).astype(jnp.bfloat16)
    return jnp.einsum('ecf,efd->ecd', hidden_act, down_full, preferred_element_type=jnp.float32).astype(jnp.bfloat16)


def local_block(hidden, norm_gain, w_router, w_gate, w_up, w_down, top2_ids):
    tok_local, d_model = hidden.shape
    num_experts = w_router.shape[1]
    capacity = (5 * tok_local + 2 * num_experts - 1) // (2 * num_experts)
    hidden_f32, normed, gate_probs = norm_and_gates(hidden, norm_gain, w_router, top2_ids)
    slot_ids = route_slots(top2_ids, num_experts, capacity)
    send_rows = gather_rows(normed, slot_ids, num_experts * capacity).reshape(num_experts, capacity, d_model)
    gate_full = lax.all_gather(w_gate, 'fsdp', axis=1, tiled=True)
    up_full = lax.all_gather(w_up, 'fsdp', axis=1, tiled=True)
    down_full = lax.all_gather(w_down, 'fsdp', axis=2, tiled=True)
    recv_rows = lax.all_to_all(send_rows, 'ep', 0, 1, tiled=True)
    expert_out = expert_block(recv_rows, gate_full, up_full, down_full)
    back_rows = lax.all_to_all(expert_out, 'ep', 1, 0, tiled=True)
    returned = take_slots(back_rows.reshape(num_experts * capacity, d_model), slot_ids)
    moe_sum = jnp.sum(gate_probs[:, :, None] * returned.astype(jnp.float32), axis=1)
    return (hidden_f32 + moe_sum).astype(jnp.bfloat16)


def solution(mesh):
    tok_spec = P(('dp', 'fsdp', 'ep'), None)
    in_specs = (tok_spec, P(None), P(None, None), P('ep', 'fsdp', None), P('ep', 'fsdp', None), P('ep', None, 'fsdp'), tok_spec)
    return jax.shard_map(local_block, mesh=mesh, in_specs=in_specs, out_specs=tok_spec, check_vma=False)
```

profile of v0, /device:TPU:0, one launch (start us, length us, event | category | flops | bytes accessed | tf_op | source)
XLA Modules:
  0.0 2119.4 jit_solution(14304843306726902140)
XLA Ops:
  6.5 0.0 copy-start
  6.5 0.7 all-gather.4.cloned.1.call-update
  7.3 0.0 copy-start.2
  7.3 0.0 all-gather.6.cloned.1.call-start
  7.3 0.7 all-gather.6.cloned.1.call-update
  8.0 0.6 copy.35
  8.7 1.2 eq.29
  9.9 1.2 eq.25
  11.1 0.1 fusion.6
  11.2 9.5 reduce-window.6
  20.8 0.9 slice_reduce_fusion
  21.7 0.2 reduce-window.9
  21.9 0.6 copy.40
  22.6 1.4 mul.59
  24.0 0.1 broadcast_in_dim.57
  24.2 1.2 reshape.148
  25.4 0.0 copy-done.9
  25.4 0.3 add_add_fusion
  25.7 0.8 fusion.5
  26.5 0.1 compare_select_fusion
  26.6 0.5 copy-done.5
  27.1 30.9 %scatter_custom_fusion = s32[10240]{0:T(1024)S(1)} fusion(s32[8192]{0:T(1024)S(1)} %bitcast.51, s32[8192]{0:T(1024)S(1)} %reshape.148, s32[]{:T(128)} %constant.68.clone.1), kind=kCustom, calls=%fused_computation.36 | custom fusion | bytes 40964 | tf_op jit(solution)/shard_map/scatter | solution.py:29
  58.1 0.1 broadcast_in_dim.58
  58.2 5.1 fusion
  63.3 7.8 fusion.2
  71.2 55.0 %gather_fusion = bf16[10240,1024]{1,0:T(8,128)(2,1)} fusion(bf16[4096,1024]{1,0:T(8,128)(2,1)} %fusion.2, s32[10240]{0:T(1024)S(1)} %fusion.7), kind=kCustom, calls=%fused_computation | custom fusion | bytes 41984000 | tf_op jit(solution)/shard_map/jit(_take)/gather | solution.py:30
  126.2 17.6 broadcast_select_fusion.1
  143.7 7.7 all-to-all-start
  151.5 0.0 all-gather.8.cloned.1.call-start
  151.5 0.7 all-gather.8.cloned.1.call-update
  152.2 227.9 %all-to-all-done = bf16[32,320,1024]{2,1,0:T(8,128)(2,1)} async-done(((bf16[32,320,1024]{2,1,0:T(8,128)(2,1)}), bf16[32,320,1024]{2,1,0:T(8,128)(2,1)}, u32[]{:S(2)}, u32[]{:S(2)}) %all-to-all-start) | async-done | bytes 20971552 | tf_op jit(solution)/shard_map/all_to_all | solution.py:54
  380.1 17.5 copy.41
  397.6 141.5 %all-gather.4.cloned.1.call-done = bf16[8,1024,2816]{2,1,0:T(8,128)(2,1)} async-done(((bf16[8,512,2816]{2,1,0:T(8,128)(2,1)}), bf16[8,1024,2816]{2,1,0:T(8,128)(2,1)}) %all-gather.4.cloned.1.call-update) | async-done | bytes 46137360 | tf_op jit(solution)/shard_map/all_gather | solution.py:51
  539.1 79.6 %fusion.15 = f32[8,1280,2816]{2,1,0:T(8,128)} fusion(bf16[8,1280,1024]{2,1,0:T(8,128)(2,1)} %bitcast.46, bf16[8,1024,2816]{2,1,0:T(8,128)(2,1)} %all-gather.4.cloned.1.call-done), kind=kOutput, calls=%fused_computation.46 | convolution fusion | flops 59055800320 | bytes 182452224 | tf_op jit(solution)/shard_map/ecd,edf->ecf/dot_general | solution.py:38
  618.7 449.4 %all-gather.6.cloned.1.call-done = bf16[8,1024,2816]{2,1,0:T(8,128)(2,1)} async-done(((bf16[8,512,2816]{2,1,0:T(8,128)(2,1)}), bf16[8,1024,2816]{2,1,0:T(8,128)(2,1)}) %all-gather.6.cloned.1.call-update) | async-done | bytes 46137360 | tf_op jit(solution)/shard_map/all_gather | solution.py:52
  1068.1 92.3 %multiply_convert_fusion.clone.4 = bf16[8,1280,2816]{2,1,0:T(8,128)(2,1)} fusion(f32[8,1280,2816]{2,1,0:T(8,128)} %fusion.15, bf16[8,1280,1024]{2,1,0:T(8,128)(2,1)} %bitcast.47, bf16[8,1024,2816]{2,1,0:T(8,128)(2,1)} %all-gather.6.cloned.1.call-done), kind=kOutput, calls=%fused_computation.4.clone.clone.clone.1 | convolution fusion | flops 59228815360 | bytes 240123904 | tf_op jit(solution)/shard_map/ecd,edf->ecf/dot_general | solution.py:39
  1160.4 437.5 %all-gather.8.cloned.1.call-done = bf16[8,2816,1024]{2,1,0:T(8,128)(2,1)} async-done(((bf16[8,2816,512]{2,1,0:T(8,128)(2,1)}), bf16[8,2816,1024]{2,1,0:T(8,128)(2,1)}) %all-gather.8.cloned.1.call-update) | async-done | bytes 46137360 | tf_op jit(solution)/shard_map/all_gather | solution.py:53
  1597.9 67.5 %convolution_convert_fusion = bf16[8,1280,1024]{2,1,0:T(8,128)(2,1)} fusion(bf16[8,2816,1024]{2,1,0:T(8,128)(2,1)} %all-gather.8.cloned.1.call-done, bf16[8,1280,2816]{2,1,0:T(8,128)(2,1)} %multiply_convert_fusion.clone.4), kind=kOutput, calls=%fused_computation.11 | convolution fusion | flops 59066286080 | bytes 124780544 | tf_op jit(solution)/shard_map/ecf,efd->ecd/dot_general | solution.py:41
  1665.4 22.8 %copy.42 = bf16[8,1280,1024]{2,0,1:T(8,128)(2,1)} copy(bf16[8,1280,1024]{2,1,0:T(8,128)(2,1)} %convolution_convert_fusion) | data formatting | bytes 41943040 | tf_op jit(solution)/shard_map/convert_element_type | solution.py:41
  1688.2 8.1 all-to-all-start.1
  1696.2 2.1 reduce_sum.43
  1698.3 0.6 copy.37
  1699.0 0.7 compare_and_fusion
  1699.6 0.6 copy.44
  1700.3 1.8 reshape.132
  1702.1 0.6 copy.32
  1702.8 1.2 reshape.138
  1704.0 0.0 copy-done
  1704.0 5.9 fusion.14
  1709.9 0.0 copy-start.4
  1710.0 65.5 %gather_fusion.2 = f32[8192]{0:T(1024)S(1)} fusion(f32[4096,32]{0,1:T(8,128)S(1)} %fusion.14, s32[8192]{0:T(1024)S(1)} %reshape.138), kind=kCustom, calls=%fused_computation.2 | custom fusion | bytes 131072 | tf_op jit(solution)/shard_map/jit(take_along_axis)/gather | solution.py:14
  1775.5 2.1 reshape.141
  1777.6 0.6 copy.33
  1778.2 0.1 fusion.13
  1778.3 0.1 fusion.11
  1778.5 0.6 copy.34
  1779.1 0.8 copy.39
  1780.0 143.9 %all-to-all-done.1 = bf16[8,1280,1024]{2,0,1:T(8,128)(2,1)} async-done(((bf16[8,1280,1024]{2,0,1:T(8,128)(2,1)}), bf16[8,1280,1024]{2,0,1:T(8,128)(2,1)}, u32[]{:S(2)}, u32[]{:S(2)}) %all-to-all-start.1) | async-done | bytes 20971552 | tf_op jit(solution)/shard_map/all_to_all | solution.py:56
  1923.9 23.0 %copy.43 = bf16[8,4,320,1024]{3,2,0,1:T(8,128)(2,1)} copy(bf16[8,4,320,1024]{3,0,2,1:T(8,128)(2,1)} %bitcast.8) | data formatting | bytes 41943040 | tf_op jit(solution)/shard_map/all_to_all | solution.py:56
  1946.9 50.3 %gather_fusion.1 = bf16[8192,1024]{1,0:T(8,128)(2,1)} fusion(bf16[10240,1024]{1,0:T(8,128)(2,1)} %bitcast.44, s32[8192]{0:T(1024)S(1)} %broadcast_clamp_fusion), kind=kCustom, calls=%fused_computation.1 | custom fusion | bytes 33587200 | tf_op jit(solution)/shard_map/jit(_take)/gather | solution.py:34
  1997.2 24.9 %reshape.131 = bf16[4096,2,1024]{2,1,0:T(2,128)(2,1)} reshape(bf16[8192,1024]{1,0:T(8,128)(2,1)} %gather_fusion.1) | data formatting | bytes 33554432 | tf_op jit(solution)/shard_map/jit(_take)/gather | solution.py:34
  2022.1 78.3 %multiply_reduce_fusion = f32[4096,1024]{1,0:T(8,128)} fusion(bf16[4096,2,1024]{2,1,0:T(2,128)(2,1)} %reshape.131, pred[4096,2]{1,0:T(8,128)(4,1)S(1)} %copy.39, f32[4096,2]{1,0:T(8,128)S(1)} %copy.34), kind=kLoop, calls=%fused_computation.5 | loop fusion | flops 29360128 | bytes 33595392 | tf_op jit(solution)/shard_map/reduce_sum | solution.py:58
  2100.4 12.0 fusion.3
  2112.4 0.0 copy-done.1
  (22 shorter events, 0.2 us)
Async XLA Ops:
  6.5 1697.5 %copy-start = (bf16[1024,32]{0,1:T(8,128)(2,1)S(1)}, bf16[1024,32]{0,1:T(8,128)(2,1)}, u32[]{:S(2)}) copy-start(bf16[1024,32]{0,1:T(8,128)(2,1)} %param.9) | copy-start | bytes 196612
  6.5 532.6 %all-gather.4.cloned.1.call-start = ((), (), s32[]{:S(2)}) async-start(), calls=%async_computation.2 | async-start | bytes 69206016 | tf_op jit(solution)/shard_map/all_gather | solution.py:51
  7.3 0.8 copy-start.2
  7.3 18.1 copy-start.9
  7.3 1060.8 %all-gather.6.cloned.1.call-start = ((), (), s32[]{:S(2)}) async-start(), calls=%async_computation.3 | async-start | bytes 69206016 | tf_op jit(solution)/shard_map/all_gather | solution.py:52
  26.5 0.6 copy-start.5
  143.7 236.3 %all-to-all-start = ((bf16[32,320,1024]{2,1,0:T(8,128)(2,1)}), bf16[32,320,1024]{2,1,0:T(8,128)(2,1)}, u32[]{:S(2)}, u32[]{:S(2)}) async-start(bf16[32,320,1024]{2,1,0:T(8,128)(2,1)} %broadcast_select_fusion.1), calls=%async_computation | async-start | bytes 41943040 | tf_op jit(solution)/shard_map/all_to_all | solution.py:54
  151.5 1446.4 %all-gather.8.cloned.1.call-start = ((), (), s32[]{:S(2)}) async-start(), calls=%async_computation.4 | async-start | bytes 69206016 | tf_op jit(solution)/shard_map/all_gather | solution.py:53
  1688.2 8.1 copy-start.6
  1688.2 10.8 copy-start.3
  1688.2 235.7 %all-to-all-start.1 = ((bf16[8,1280,1024]{2,0,1:T(8,128)(2,1)}), bf16[8,1280,1024]{2,0,1:T(8,128)(2,1)}, u32[]{:S(2)}, u32[]{:S(2)}) async-start(bf16[8,1280,1024]{2,0,1:T(8,128)(2,1)} %copy.42), calls=%async_computation.1 | async-start | bytes 41943040 | tf_op jit(solution)/shard_map/all_to_all | solution.py:56
  1709.9 68.3 %copy-start.4 = (s32[4096,2]{0,1:T(2,128)S(1)}, s32[4096,2]{0,1:T(2,128)}, u32[]{:S(2)}) copy-start(s32[4096,2]{0,1:T(2,128)} %param.13) | copy-start | bytes 98308
  1710.0 69.1 %copy-start.8 = (pred[4096,2]{0,1:T(4,128)(4,1)S(1)}, pred[4096,2]{0,1:T(4,128)(4,1)}, u32[]{:S(2)}) copy-start(pred[4096,2]{0,1:T(4,128)(4,1)} %get-tuple-element.7) | copy-start | bytes 24580
  1710.0 70.0 %copy-start.7 = (s32[8192]{0:T(1024)S(1)}, s32[8192]{0:T(1024)}, u32[]{:S(2)}) copy-start(s32[8192]{0:T(1024)} %reshape.132) | copy-start | bytes 98308
  2022.1 90.3 %copy-start.1 = (bf16[1024,32]{0,1:T(8,128)(2,1)S(1)}, bf16[1024,32]{0,1:T(8,128)(2,1)}, u32[]{:S(2)}) copy-start(bf16[1024,32]{0,1:T(8,128)(2,1)} %param.9) | copy-start | bytes 196612
Sparse Core Ops, SparseCore 0:
  8.8 530.2 all-gather.3
  540.6 527.4 all-gather.5
  1069.7 528.1 all-gather.7
where the time goes:
time: 2130 us; the launch traced here: 2120 us
  waiting for transfers between devices  1400 us (66%)
  local copies, waits for them, and re-layouts  309 us (15%)
  matrix products  245 us (12%)
  other arithmetic  133 us (6%)
    all_gather x1, waiting for transfers between devices, local_block(): up_full = lax.all_gather(w_up, 'fsdp', axis=1, tiled=True)  449 us
    all_gather x1, waiting for transfers between devices, local_block(): down_full = lax.all_gather(w_down, 'fsdp', axis=2, tiled=True)  437 us
    all_to_all x1, waiting for transfers between devices, local_block(): recv_rows = lax.all_to_all(send_rows, 'ep', 0, 1, tiled=True)  228 us
    all_to_all x1, waiting for transfers between devices, local_block(): back_rows = lax.all_to_all(expert_out, 'ep', 1, 0, tiled=True)  144 us
    all_gather x1, waiting for transfers between devices, local_block(): gate_full = lax.all_gather(w_gate, 'fsdp', axis=1, tiled=True)  142 us
    dot_general x1, matrix products, expert_block(): jnp.einsum('ecd,edf->ecf', rows_in, up_full, preferred_element_type=jnp.f...  92.3 us
    dot_general x1, matrix products, expert_block(): jnp.einsum('ecd,edf->ecf', rows_in, gate_full, preferred_element_type=jnp...  79.6 us
    reduce_sum x1, other arithmetic, local_block(): jnp.sum(gate_probs[:, :, None] * returned.astype(jnp.float32), axis=1)  78.3 us
  transfers between devices with their start and end apart: 5, of which 5 were waited for; matrix products, arithmetic and copies ran while one was open for 19% of the time, Pallas kernels for 0%

commit v1 on v0

v1 whole, which is shorter than its diff:
```python
import functools

import jax
import jax.numpy as jnp
from jax import lax
from jax.experimental import pallas as pl
from jax.experimental.pallas import tpu as pltpu
from jax.sharding import PartitionSpec as P

EPS = 1e-5
MESH = pl.DeviceIdType.MESH
F32 = jnp.float32
BF16 = jnp.bfloat16


def iota(shape, dim):
    return lax.broadcasted_iota(jnp.int32, shape, dim)


def moe_kernel(cfg, hid, gain, wr, wg, wu, wd, ids_row, ids_col,
               out, rhid, rg, ru, rd, stage, rows, ostage, ret,
               big, vg, vu, vd, acc, hbuf, obuf, gbuf, rbuf, ohbuf, meta, srow, rids,
               lsem, wl_sem, out_sem, ids_sem, hid_sem, w_ssem, w_rsem,
               row_ssem, row_rsem, ret_ssem, ret_rsem):
    nf, nj, per, cap, tok, dm, ff, ne = cfg
    half = dm // nf
    ndev = nf * nj
    f = lax.axis_index('fsdp')
    j = lax.axis_index('ep')
    me = f * nj + j
    of = 1 - f
    peer = {'fsdp': of, 'ep': j}

    barrier = pltpu.get_barrier_semaphore()

    @pl.loop(1, ndev)
    def _(d):
        t = lax.rem(me + d, ndev)
        pl.semaphore_signal(barrier, inc=1, device_id={'fsdp': t // nj, 'ep': lax.rem(t, nj)}, device_id_type=MESH)
    pl.semaphore_wait(barrier, ndev - 1)

    def to_peer(src, dst, s_sem, r_sem):
        return pltpu.make_async_remote_copy(src_ref=src, dst_ref=dst, send_sem=s_sem, recv_sem=r_sem,
                                            device_id=peer, device_id_type=MESH)

    ids_copy = to_peer(ids_row, rids, ids_sem.at[0], ids_sem.at[1])
    hid_copy = to_peer(hid, rhid, hid_sem.at[0], hid_sem.at[1])

    def weight_copies(i):
        return [to_peer(src.at[per * of + i], dst.at[i], w_ssem.at[3 * i + m], w_rsem.at[3 * i + m])
                for m, (src, dst) in enumerate(((wg, rg), (wu, ru), (wd, rd)))]

    ids_copy.start()
    hid_copy.start()

    @pl.loop(0, per)
    def _(i):
        for copy in weight_copies(i):
            copy.start()

    load = pltpu.make_async_copy(hid, big, lsem)
    load.start()
    load.wait()
    tt = min(256, tok)
    gain_f = gain[...].astype(F32)

    def normed_tile(rows_at):
        x = big[rows_at, :].astype(F32)
        mean_sq = jnp.mean(x * x, axis=-1, keepdims=True)
        u = (x * lax.rsqrt(mean_sq + EPS) * gain_f).astype(BF16)
        big[rows_at, :] = u
        return x, u

    lower = jnp.where(iota((tt, tt), 0) > iota((tt, tt), 1), 1.0, 0.0).astype(BF16)
    upper = jnp.where(iota((tt, tt), 0) < iota((tt, tt), 1), 1.0, 0.0).astype(BF16)

    def own_tile(t, carry):
        at = pl.ds(pl.multiple_of(t * tt, tt), tt)
        x, u = normed_tile(at)
        acc[at, :] = x
        logits = jnp.dot(u, wr[...], preferred_element_type=F32)
        lane = iota((tt, 128), 1)
        ids = ids_col[at, :]
        pick = [lane == ids[:, k:k + 1] for k in range(2)]
        count = jnp.where(pick[0] | pick[1], 1.0, 0.0)
        pos = jnp.dot(lower, count.astype(BF16), preferred_element_type=F32) + carry
        slot, score = [], []
        for k in range(2):
            place = jnp.sum(jnp.where(pick[k], pos, 0.0), axis=1, keepdims=True)
            slot.append(jnp.where(place < cap, ids[:, k:k + 1].astype(F32) * cap + place, -1.0))
            score.append(jnp.sum(jnp.where(pick[k], logits, 0.0), axis=1, keepdims=True))
        top = jnp.maximum(score[0], score[1])
        ex = [jnp.exp(s - top) for s in score]
        gate = [e / (ex[0] + ex[1]) for e in ex]
        meta[at, :] = jnp.where(lane == 0, slot[0], jnp.where(lane == 1, slot[1], jnp.where(lane == 2, gate[0], gate[1])))
        return carry + jnp.sum(count, axis=0, keepdims=True)

    lax.fori_loop(0, tok // tt, own_tile, jnp.zeros((1, 128), F32))

    def slot_rows(ids_ref):
        def tile(t, carry):
            at = pl.ds(pl.multiple_of(t * tt, tt), tt)
            sub = iota((ne, tt), 0)
            ids = [ids_ref[k:k + 1, at] for k in range(2)]
            pick = [sub == e for e in ids]
            count = jnp.where(pick[0] | pick[1], 1.0, 0.0)
            pos = jnp.dot(count.astype(BF16), upper, preferred_element_type=F32) + carry
            for k in range(2):
                place = jnp.sum(jnp.where(pick[k], pos, 0.0), axis=0, keepdims=True)
                srow[k:k + 1, at] = jnp.where(place < cap, ids[k].astype(F32) * cap + place, -1.0)
            return carry + jnp.sum(count, axis=1, keepdims=True)
        lax.fori_loop(0, tok // tt, tile, jnp.zeros((ne, 1), F32))

    tk = min(512, tok)
    tn = 256

    def pick_and_send(src, src_idx):
        @pl.loop(0, nj * per)
        def _(n):
            d, i = n // per, lax.rem(n, per)
            jo = lax.rem(j + d, nj)
            base = ((jo * nf + f) * per + i) * cap

            @pl.loop(0, tok // tk)
            def _(t):
                at = pl.ds(pl.multiple_of(t * tk, tk), tk)
                sub = iota((cap, tk), 0)
                s0 = srow[0:1, at].astype(jnp.int32) - base
                s1 = srow[1:2, at].astype(jnp.int32) - base
                ohbuf[:, at] = jnp.where((sub == s0) | (sub == s1), 1.0, 0.0).astype(BF16)

            @pl.loop(0, dm // tn)
            def _(t):
                at = pl.ds(pl.multiple_of(t * tn, tn), tn)
                gbuf[:, at] = jnp.dot(ohbuf[...], big[:, at], preferred_element_type=F32).astype(BF16)

            place = pl.ds(pl.multiple_of(src_idx * cap, cap), cap)

            @pl.when(d == 0)
            def _():
                copy = pltpu.make_async_copy(gbuf, rows.at[i, place], lsem)
                copy.start()
                copy.wait()

            @pl.when(d > 0)
            def _():
                k = src * nj * per + n
                copy = pltpu.make_async_copy(gbuf, stage.at[k], lsem)
                copy.start()
                copy.wait()
                pltpu.make_async_remote_copy(
                    src_ref=stage.at[k], dst_ref=rows.at[i, place], send_sem=row_ssem.at[k],
                    recv_sem=row_rsem.at[i * ndev + src_idx],
                    device_id={'fsdp': f, 'ep': jo}, device_id_type=MESH).start()

    slot_rows(ids_row)
    pick_and_send(0, me)

    ids_copy.wait()
    hid_copy.wait()
    load = pltpu.make_async_copy(rhid, big, lsem)
    load.start()
    load.wait()

    @pl.loop(0, tok // tt)
    def _(t):
        normed_tile(pl.ds(pl.multiple_of(t * tt, tt), tt))
    slot_rows(rids)
    pick_and_send(1, of * nj + j)

    tc = min(512, tok)

    def combine(fo, jo, i):
        e = (jo * nf + fo) * per + i

        @pl.when(fo * nj + jo != me)
        def _():
            pltpu.make_async_copy(ret.at[e], ret.at[e], ret_rsem.at[e]).wait()
        fetch = pltpu.make_async_copy(ret.at[e], rbuf, lsem)
        fetch.start()
        fetch.wait()

        @pl.loop(0, tok // tc)
        def _(t):
            at = pl.ds(pl.multiple_of(t * tc, tc), tc)
            base = (e * cap).astype(F32)
            m = meta[at, :]
            s0, s1 = m[:, 0:1] - base, m[:, 1:2] - base
            in0 = (s0 >= 0) & (s0 < cap)
            in1 = (s1 >= 0) & (s1 < cap)
            gate = jnp.where(in0, m[:, 2:3], jnp.where(in1, m[:, 3:4], 0.0))
            lane = iota((tc, cap), 1)
            hot = jnp.where((lane == s0.astype(jnp.int32)) | (lane == s1.astype(jnp.int32)), 1.0, 0.0).astype(BF16)
            acc[at, :] += gate * jnp.dot(hot, rbuf[...], preferred_element_type=F32)

    pair = 2 * cap

    @pl.loop(0, per)
    def _(i):
        mine = pl.ds(pl.multiple_of(f * half, half), half)
        theirs = pl.ds(pl.multiple_of(of * half, half), half)
        own = [pltpu.make_async_copy(wg.at[per * f + i], vg.at[mine], wl_sem.at[0]),
               pltpu.make_async_copy(wu.at[per * f + i], vu.at[mine], wl_sem.at[1]),
               pltpu.make_async_copy(wd.at[per * f + i], vd.at[:, mine], wl_sem.at[2])]
        for copy in own:
            copy.start()

        @pl.loop(0, ndev)
        def _(s):
            @pl.when(lax.rem(s, nj) != j)
            def _():
                block = rows.at[i, pl.ds(pl.multiple_of(s * cap, cap), cap)]
                pltpu.make_async_copy(block, block, row_rsem.at[i * ndev + s]).wait()
        tokens = pltpu.make_async_copy(rows.at[i], big.at[pl.ds(0, ndev * cap)], lsem)
        tokens.start()
        got = [pltpu.make_async_copy(rg.at[i], vg.at[theirs], wl_sem.at[3]),
               pltpu.make_async_copy(ru.at[i], vu.at[theirs], wl_sem.at[4]),
               pltpu.make_async_copy(rd.at[i], vd.at[:, theirs], wl_sem.at[5])]
        for remote, copy in zip(weight_copies(i), got):
            remote.wait_recv()
            copy.start()
        tokens.wait()
        for copy in own + got:
            copy.wait()

        @pl.loop(0, ndev // 2)
        def _(p):
            xs = pl.ds(pl.multiple_of(p * pair, pair), pair)

            @pl.loop(0, ff // tn)
            def _(t):
                at = pl.ds(pl.multiple_of(t * tn, tn), tn)
                a = jnp.dot(big[xs, :], vg[:, at], preferred_element_type=F32)
                b = jnp.dot(big[xs, :], vu[:, at], preferred_element_type=F32)
                hbuf[:, at] = (a * jax.nn.sigmoid(a) * b).astype(BF16)

            @pl.loop(0, dm // tn)
            def _(t):
                at = pl.ds(pl.multiple_of(t * tn, tn), tn)
                obuf[:, at] = jnp.dot(hbuf[...], vd[:, at], preferred_element_type=F32).astype(BF16)

            e = (j * nf + f) * per + i
            for q in range(2):
                s = 2 * p + q
                part = obuf.at[pl.ds(q * cap, cap)]

                @pl.when(s == me)
                def _():
                    copy = pltpu.make_async_copy(part, ret.at[e], lsem)
                    copy.start()
                    copy.wait()

                @pl.when(s != me)
                def _():
                    k = i * ndev + s
                    copy = pltpu.make_async_copy(part, ostage.at[k], lsem)
                    copy.start()
                    copy.wait()
                    pltpu.make_async_remote_copy(
                        src_ref=ostage.at[k], dst_ref=ret.at[e], send_sem=ret_ssem.at[k],
                        recv_sem=ret_rsem.at[e],
                        device_id={'fsdp': s // nj, 'ep': lax.rem(s, nj)}, device_id_type=MESH).start()

        @pl.loop(0, nj)
        def _(d):
            combine(f, lax.rem(j + d, nj), i)

    @pl.loop(0, nj * per)
    def _(n):
        combine(of, lax.rem(j + lax.rem(n, nj), nj), n // nj)

    def out_copy(t):
        at = pl.ds(pl.multiple_of(t * tc, tc), tc)
        return pltpu.make_async_copy(big.at[at], out.at[at], out_sem.at[t])

    @pl.loop(0, tok // tc)
    def _(t):
        at = pl.ds(pl.multiple_of(t * tc, tc), tc)
        big[at, :] = acc[at, :].astype(BF16)
        out_copy(t).start()

    @pl.loop(0, tok // tc)
    def _(t):
        out_copy(t).wait()

    @pl.loop(0, per)
    def _(i):
        for copy in weight_copies(i):
            copy.wait_send()

    @pl.loop(0, 2 * nj * per)
    def _(k):
        @pl.when(lax.rem(k, nj * per) >= per)
        def _():
            pltpu.make_async_copy(stage.at[k], stage.at[k], row_ssem.at[k]).wait()

    @pl.loop(0, per * ndev)
    def _(k):
        @pl.when(lax.rem(k, ndev) != me)
        def _():
            pltpu.make_async_copy(ostage.at[k], ostage.at[k], ret_ssem.at[k]).wait()


def local_block(nf, nj, hidden, norm_gain, w_router, w_gate, w_up, w_down, top2_ids):
    tok, dm = hidden.shape
    ne = w_router.shape[1]
    per = ne // (nf * nj)
    ff = w_gate.shape[2]
    cap = (5 * tok + 2 * ne - 1) // (2 * ne)
    ndev = nf * nj
    half = dm // nf
    cfg = (nf, nj, per, cap, tok, dm, ff, ne)
    ids_row = jnp.pad(top2_ids.T, ((0, 6), (0, 0)))
    router = jnp.pad(w_router, ((0, 0), (0, 128 - ne)))
    sds = jax.ShapeDtypeStruct
    anyspec = pl.BlockSpec(memory_space=pl.ANY)
    vspec = pl.BlockSpec(memory_space=pltpu.VMEM)
    outs = [
        sds((tok, dm), BF16), sds((tok, dm), BF16),
        sds((per, half, ff), BF16), sds((per, half, ff), BF16), sds((per, ff, half), BF16),
        sds((2 * nj * per, cap, dm), BF16), sds((per, ndev * cap, dm), BF16),
        sds((per * ndev, cap, dm), BF16), sds((ne, cap, dm), BF16),
    ]
    dma = pltpu.SemaphoreType.DMA
    scratch = [
        pltpu.VMEM((tok, dm), BF16),
        pltpu.VMEM((dm, ff), BF16), pltpu.VMEM((dm, ff), BF16), pltpu.VMEM((ff, dm), BF16),
        pltpu.VMEM((tok, dm), F32),
        pltpu.VMEM((2 * cap, ff), BF16), pltpu.VMEM((2 * cap, dm), BF16),
        pltpu.VMEM((cap, dm), BF16), pltpu.VMEM((cap, dm), BF16), pltpu.VMEM((cap, tok), BF16),
        pltpu.VMEM((tok, 128), F32), pltpu.VMEM((8, tok), F32), pltpu.VMEM((8, tok), jnp.int32),
        dma, dma((6,)), dma((8,)), dma((2,)), dma((2,)), dma((3 * per,)), dma((3 * per,)),
        dma((2 * nj * per,)), dma((per * ndev,)), dma((per * ndev,)), dma((ne,)),
    ]
    flops = 6 * per * ndev * cap * dm * ff + 3 * 2 * ne * cap * tok * dm
    result = pl.pallas_call(
        functools.partial(moe_kernel, cfg),
        out_shape=outs,
        in_specs=[anyspec, vspec, vspec, anyspec, anyspec, anyspec, vspec, vspec],
        out_specs=[anyspec] * len(outs),
        scratch_shapes=scratch,
        compiler_params=pltpu.CompilerParams(collective_id=0, has_side_effects=True, vmem_limit_bytes=67043328),
        cost_estimate=pl.CostEstimate(flops=flops, bytes_accessed=400 * 1024 * 1024, transcendentals=0),
        name='moe_block',
    )(hidden, norm_gain.reshape(1, dm), router, w_gate, w_up, w_down, ids_row, top2_ids)
    return result[0]


def solution(mesh):
    tok_spec = P(('dp', 'fsdp', 'ep'), None)
    in_specs = (tok_spec, P(None), P(None, None), P('ep', 'fsdp', None), P('ep', 'fsdp', None), P('ep', None, 'fsdp'), tok_spec)
    body = functools.partial(local_block, mesh.shape['fsdp'], mesh.shape['ep'])
    return jax.shard_map(body, mesh=mesh, in_specs=in_specs, out_specs=tok_spec, check_vma=False)
```

time: 2130 us -> 1280 us (0.60)
  waiting for transfers between devices: 1400 us -> 0 us
  Pallas kernels: 0 us -> 1240 us
  local copies, waits for them, and re-layouts: 309 us -> 15 us
  matrix products: 245 us -> 0 us
  other arithmetic: 133 us -> 0 us
    pallas_call x0 -> x1, Pallas kernels: none -> 1240 us  [local_block(): pl.pallas_call(functools.partial(moe_kernel, cfg), out_shape=outs, in_spe...]
    all_gather x3 -> x0, waiting for transfers between devices: 1030 us -> none  [the longest x1 449 us: local_block(): up_full = lax.all_gather(w_up, 'fsdp', axis=1, tiled=True)]
    all_to_all x2 -> x0, waiting for transfers between devices: 372 us -> none  [the longest x1 228 us: local_block(): recv_rows = lax.all_to_all(send_rows, 'ep', 0, 1, tiled=True)]
    dot_general x4 -> x0, matrix products: 245 us -> none  [the longest x1 92.3 us: expert_block(): jnp.einsum('ecd,edf->ecf', rows_in, up_full, preferred_element_type=jnp.f...]
    gather x8 -> x0, local copies, waits for them, and re-layouts: 200 us -> none  [the longest x2 75.2 us: take_slots(): return jnp.take(expert_rows, slot_ids, axis=0, mode='fill', fill_value=0)]
    reduce_sum x4 -> x0, other arithmetic: 84.3 us -> none  [the longest x1 78.3 us: local_block(): jnp.sum(gate_probs[:, :, None] * returned.astype(jnp.float32), axis=1)]
    all_to_all x2 -> x0, local copies, waits for them, and re-layouts: 40.5 us -> none  [the longest x1 23 us: local_block(): back_rows = lax.all_to_all(expert_out, 'ep', 1, 0, tiled=True)]
    scatter x1 -> x0, local copies, waits for them, and re-layouts: 30.9 us -> none  [gather_rows(): jnp.full((num_slots,), tok_count, dtype=jnp.int32).at[slot_ids.reshape(-1)]]
  transfers between devices with their start and end apart: 5 -> 0, of which waited for: 5 -> 0; matrix products, arithmetic and copies ran while one was open for 19% -> 0% of each run, Pallas kernels for 0% -> 0%
where the time goes in v1:
time: 1280 us; the launch traced here: 1260 us
  Pallas kernels  1240 us (97%)
  local copies, waits for them, and re-layouts  15 us (1%)
    pallas_call x1, Pallas kernels, local_block(): pl.pallas_call(functools.partial(moe_kernel, cfg), out_shape=outs, in_spe...  1240 us

profile of v1, /device:TPU:0, one launch (start us, length us, event | category | flops | bytes accessed | tf_op | source)
XLA Modules:
  0.0 1255.2 jit_solution(735225894840199105)
XLA Ops:
  0.0 1.3 reshape.3.gain
  1.3 1.4 pad.9.ids_row
  2.7 1.0 copy.8
  3.7 0.8 pad.8.wr
  4.5 2.7 copy.9.ids_col
  7.2 1240.2 %moe_block.1 = (bf16[4096,1024]{1,0:T(8,128)(2,1)}, bf16[4096,1024]{1,0:T(8,128)(2,1)}, bf16[4,512,2816]{2,1,0:T(8,128)(2,1)}, bf16[4,512,2816]{2,1,0:T(8,128)(2...) custom-call(bf16[4096,1024]{1,0:T(8,128)(2,1)} %hid.1, ...), custom_call_target="tpu_custom_call" | custom-call | flops 434865438720 | bytes 419430400 | tf_op jit(solution)/shard_map/moe_block/pallas_call | solution.py:336
  1247.4 7.8 copy.11

commit v2 on v1

--- a/solution.py
+++ b/solution.py
@@ -17,10 +17,10 @@
     return lax.broadcasted_iota(jnp.int32, shape, dim)
 
 
-def moe_kernel(cfg, hid, gain, wr, wg, wu, wd, ids_row, ids_col,
+def moe_kernel(cfg, hid, gain, wr, wg, wu, wd, ids_row,
                out, rhid, rg, ru, rd, stage, rows, ostage, ret,
                big, vg, vu, vd, acc, hbuf, obuf, gbuf, rbuf, ohbuf, meta, srow, rids,
-               lsem, wl_sem, out_sem, ids_sem, hid_sem, w_ssem, w_rsem,
+               lsem, wl_sem, tok_sem, out_sem, ids_sem, hid_sem, w_ssem, w_rsem,
                row_ssem, row_rsem, ret_ssem, ret_rsem):
     nf, nj, per, cap, tok, dm, ff, ne = cfg
     half = dm // nf
@@ -62,6 +62,7 @@
     load.start()
     load.wait()
     tt = min(256, tok)
+    router = jnp.concatenate([wr[...], jnp.zeros((128 - ne, dm), BF16)], axis=0)
     gain_f = gain[...].astype(F32)
 
     def normed_tile(rows_at):
@@ -71,31 +72,7 @@
         big[rows_at, :] = u
         return x, u
 
-    lower = jnp.where(iota((tt, tt), 0) > iota((tt, tt), 1), 1.0, 0.0).astype(BF16)
     upper = jnp.where(iota((tt, tt), 0) < iota((tt, tt), 1), 1.0, 0.0).astype(BF16)
-
-    def own_tile(t, carry):
-        at = pl.ds(pl.multiple_of(t * tt, tt), tt)
-        x, u = normed_tile(at)
-        acc[at, :] = x
-        logits = jnp.dot(u, wr[...], preferred_element_type=F32)
-        lane = iota((tt, 128), 1)
-        ids = ids_col[at, :]
-        pick = [lane == ids[:, k:k + 1] for k in range(2)]
-        count = jnp.where(pick[0] | pick[1], 1.0, 0.0)
-        pos = jnp.dot(lower, count.astype(BF16), preferred_element_type=F32) + carry
-        slot, score = [], []
-        for k in range(2):
-            place = jnp.sum(jnp.where(pick[k], pos, 0.0), axis=1, keepdims=True)
-            slot.append(jnp.where(place < cap, ids[:, k:k + 1].astype(F32) * cap + place, -1.0))
-            score.append(jnp.sum(jnp.where(pick[k], logits, 0.0), axis=1, keepdims=True))
-        top = jnp.maximum(score[0], score[1])
-        ex = [jnp.exp(s - top) for s in score]
-        gate = [e / (ex[0] + ex[1]) for e in ex]
-        meta[at, :] = jnp.where(lane == 0, slot[0], jnp.where(lane == 1, slot[1], jnp.where(lane == 2, gate[0], gate[1])))
-        return carry + jnp.sum(count, axis=0, keepdims=True)
-
-    lax.fori_loop(0, tok // tt, own_tile, jnp.zeros((1, 128), F32))
 
     def slot_rows(ids_ref):
         def tile(t, carry):
@@ -111,6 +88,24 @@
             return carry + jnp.sum(count, axis=1, keepdims=True)
         lax.fori_loop(0, tok // tt, tile, jnp.zeros((ne, 1), F32))
 
+    def own_tile(t):
+        at = pl.ds(pl.multiple_of(t * tt, tt), tt)
+        x, u = normed_tile(at)
+        acc[at, :] = x
+        logits = lax.dot_general(u, router, (((1,), (1,)), ((), ())), preferred_element_type=F32)
+        lane = iota((tt, 128), 1)
+        eye = iota((tt, tt), 0) == iota((tt, tt), 1)
+
+        def column(row):
+            return jnp.sum(jnp.where(eye, row, 0.0), axis=1, keepdims=True)
+        slot = [column(srow[k:k + 1, at]) for k in range(2)]
+        ids = [column(ids_row[k:k + 1, at].astype(F32)).astype(jnp.int32) for k in range(2)]
+        score = [jnp.sum(jnp.where(lane == e, logits, 0.0), axis=1, keepdims=True) for e in ids]
+        top = jnp.maximum(score[0], score[1])
+        ex = [jnp.exp(v - top) for v in score]
+        gate = [v / (ex[0] + ex[1]) for v in ex]
+        meta[at, :] = jnp.where(lane == 0, slot[0], jnp.where(lane == 1, slot[1], jnp.where(lane == 2, gate[0], gate[1])))
+
     tk = min(512, tok)
     tn = 256
 
@@ -154,6 +149,7 @@
                     device_id={'fsdp': f, 'ep': jo}, device_id_type=MESH).start()
 
     slot_rows(ids_row)
+    pl.loop(0, tok // tt)(own_tile)
     pick_and_send(0, me)
 
     ids_copy.wait()
@@ -170,7 +166,11 @@
 
     tc = min(512, tok)
 
-    def combine(fo, jo, i):
+    def out_copy(t):
+        at = pl.ds(pl.multiple_of(t * tc, tc), tc)
+        return pltpu.make_async_copy(big.at[at], out.at[at], out_sem.at[t])
+
+    def combine(fo, jo, i, last=False):
         e = (jo * nf + fo) * per + i
 
         @pl.when(fo * nj + jo != me)
@@ -191,9 +191,17 @@
             gate = jnp.where(in0, m[:, 2:3], jnp.where(in1, m[:, 3:4], 0.0))
             lane = iota((tc, cap), 1)
             hot = jnp.where((lane == s0.astype(jnp.int32)) | (lane == s1.astype(jnp.int32)), 1.0, 0.0).astype(BF16)
-            acc[at, :] += gate * jnp.dot(hot, rbuf[...], preferred_element_type=F32)
+            total = acc[at, :] + gate * jnp.dot(hot, rbuf[...], preferred_element_type=F32)
+            if last:
+                big[at, :] = total.astype(BF16)
+                out_copy(t).start()
+            else:
+                acc[at, :] = total
 
     pair = 2 * cap
+
+    def source(n):
+        return jnp.where(n < nj, of, f) * nj + lax.rem(j + n, nj)
 
     @pl.loop(0, per)
     def _(i):
@@ -205,21 +213,29 @@
         for copy in own:
             copy.start()
 
+        def tokens(n):
+            return pltpu.make_async_copy(rows.at[i, pl.ds(pl.multiple_of(source(n) * cap, cap), cap)],
+                                         big.at[pl.ds(pl.multiple_of(n * cap, cap), cap)], tok_sem.at[n])
+
         @pl.loop(0, ndev)
-        def _(s):
+        def _(n):
+            s = source(n)
+
             @pl.when(lax.rem(s, nj) != j)
             def _():
                 block = rows.at[i, pl.ds(pl.multiple_of(s * cap, cap), cap)]
                 pltpu.make_async_copy(block, block, row_rsem.at[i * ndev + s]).wait()
-        tokens = pltpu.make_async_copy(rows.at[i], big.at[pl.ds(0, ndev * cap)], lsem)
-        tokens.start()
+            tokens(n).start()
         got = [pltpu.make_async_copy(rg.at[i], vg.at[theirs], wl_sem.at[3]),
                pltpu.make_async_copy(ru.at[i], vu.at[theirs], wl_sem.at[4]),
                pltpu.make_async_copy(rd.at[i], vd.at[:, theirs], wl_sem.at[5])]
         for remote, copy in zip(weight_copies(i), got):
             remote.wait_recv()
             copy.start()
-        tokens.wait()
+
+        @pl.loop(0, ndev)
+        def _(n):
+            tokens(n).wait()
         for copy in own + got:
             copy.wait()
 
@@ -241,7 +257,7 @@
 
             e = (j * nf + f) * per + i
             for q in range(2):
-                s = 2 * p + q
+                s = source(2 * p + q)
                 part = obuf.at[pl.ds(q * cap, cap)]
 
                 @pl.when(s == me)
@@ -263,21 +279,12 @@
 
         @pl.loop(0, nj)
         def _(d):
-            combine(f, lax.rem(j + d, nj), i)
-
-    @pl.loop(0, nj * per)
+            combine(f, lax.rem(j + nj - d, nj), i)
+
+    @pl.loop(0, nj * per - 1)
     def _(n):
-        combine(of, lax.rem(j + lax.rem(n, nj), nj), n // nj)
-
-    def out_copy(t):
-        at = pl.ds(pl.multiple_of(t * tc, tc), tc)
-        return pltpu.make_async_copy(big.at[at], out.at[at], out_sem.at[t])
-
-    @pl.loop(0, tok // tc)
-    def _(t):
-        at = pl.ds(pl.multiple_of(t * tc, tc), tc)
-        big[at, :] = acc[at, :].astype(BF16)
-        out_copy(t).start()
+        combine(of, lax.rem(j + nj - lax.rem(n, nj), nj), n // nj)
+    combine(of, lax.rem(j + 1, nj), per - 1, last=True)
 
     @pl.loop(0, tok // tc)
     def _(t):
@@ -310,8 +317,6 @@
     ndev = nf * nj
     half = dm // nf
     cfg = (nf, nj, per, cap, tok, dm, ff, ne)
-    ids_row = jnp.pad(top2_ids.T, ((0, 6), (0, 0)))
-    router = jnp.pad(w_router, ((0, 0), (0, 128 - ne)))
     sds = jax.ShapeDtypeStruct
     anyspec = pl.BlockSpec(memory_space=pl.ANY)
     vspec = pl.BlockSpec(memory_space=pltpu.VMEM)
@@ -328,21 +333,21 @@
         pltpu.VMEM((tok, dm), F32),
         pltpu.VMEM((2 * cap, ff), BF16), pltpu.VMEM((2 * cap, dm), BF16),
         pltpu.VMEM((cap, dm), BF16), pltpu.VMEM((cap, dm), BF16), pltpu.VMEM((cap, tok), BF16),
-        pltpu.VMEM((tok, 128), F32), pltpu.VMEM((8, tok), F32), pltpu.VMEM((8, tok), jnp.int32),
-        dma, dma((6,)), dma((8,)), dma((2,)), dma((2,)), dma((3 * per,)), dma((3 * per,)),
+        pltpu.VMEM((tok, 128), F32), pltpu.VMEM((8, tok), F32), pltpu.VMEM((2, tok), jnp.int32),
+        dma, dma((6,)), dma((ndev,)), dma((8,)), dma((2,)), dma((2,)), dma((3 * per,)), dma((3 * per,)),
         dma((2 * nj * per,)), dma((per * ndev,)), dma((per * ndev,)), dma((ne,)),
     ]
     flops = 6 * per * ndev * cap * dm * ff + 3 * 2 * ne * cap * tok * dm
     result = pl.pallas_call(
         functools.partial(moe_kernel, cfg),
         out_shape=outs,
-        in_specs=[anyspec, vspec, vspec, anyspec, anyspec, anyspec, vspec, vspec],
+        in_specs=[anyspec, vspec, vspec, anyspec, anyspec, anyspec, vspec],
         out_specs=[anyspec] * len(outs),
         scratch_shapes=scratch,
         compiler_params=pltpu.CompilerParams(collective_id=0, has_side_effects=True, vmem_limit_bytes=67043328),
         cost_estimate=pl.CostEstimate(flops=flops, bytes_accessed=400 * 1024 * 1024, transcendentals=0),
         name='moe_block',
-    )(hidden, norm_gain.reshape(1, dm), router, w_gate, w_up, w_down, ids_row, top2_ids)
+    )(hidden, norm_gain.reshape(1, dm), w_router.T, w_gate, w_up, w_down, top2_ids.T)
     return result[0]
 
 

time: 1280 us -> 1250 us (0.977); the launches traced: 1260 us -> 1240 us
  no operation moved by 1% of the time
where the time goes in v2:
time: 1250 us; the launch traced here: 1240 us
  Pallas kernels  1230 us (98%)
    pallas_call x1, Pallas kernels, local_block(): pl.pallas_call(functools.partial(moe_kernel, cfg), out_shape=outs, in_spe...  1230 us

profile of v2, /device:TPU:0, one launch (start us, length us, event | category | flops | bytes accessed | tf_op | source)
XLA Modules:
  0.0 1243.9 jit_solution(3041674179402769927)
XLA Ops:
  0.0 1.3 reshape.3.gain
  1.3 1234.9 %moe_block.1 = (bf16[4096,1024]{1,0:T(8,128)(2,1)}, bf16[4096,1024]{1,0:T(8,128)(2,1)}, bf16[4,512,2816]{2,1,0:T(8,128)(2,1)}, bf16[4,512,2816]{2,1,0:T(8,128)(2...) custom-call(bf16[4096,1024]{1,0:T(8,128)(2,1)} %hid.1, ...), custom_call_target="tpu_custom_call" | custom-call | flops 434865438720 | bytes 419430400 | tf_op jit(solution)/shard_map/moe_block/pallas_call | solution.py:341
  1236.2 7.8 copy.9

commit v3 on v2

--- a/solution.py
+++ b/solution.py
@@ -17,8 +17,25 @@
     return lax.broadcasted_iota(jnp.int32, shape, dim)
 
 
+def add_expert(total, m, block, e, cap):
+    base = (e * cap).astype(F32)
+    s0, s1 = m[:, 0:1] - base, m[:, 1:2] - base
+    in0 = (s0 >= 0) & (s0 < cap)
+    in1 = (s1 >= 0) & (s1 < cap)
+    gate = jnp.where(in0, m[:, 2:3], jnp.where(in1, m[:, 3:4], 0.0))
+    lane = iota((m.shape[0], cap), 1)
+    hot = jnp.where((lane == s0.astype(jnp.int32)) | (lane == s1.astype(jnp.int32)), 1.0, 0.0).astype(BF16)
+    return total + gate * jnp.dot(hot, block, preferred_element_type=F32)
+
+
+def last_kernel(nf, nj, per, cap, acc, meta, ret, out):
+    f, j = lax.axis_index('fsdp'), lax.axis_index('ep')
+    e = (lax.rem(j + 1, nj) * nf + 1 - f) * per + per - 1
+    out[...] = add_expert(acc[...], meta[...], ret[0], e, cap).astype(BF16)
+
+
 def moe_kernel(cfg, hid, gain, wr, wg, wu, wd, ids_row,
-               out, rhid, rg, ru, rd, stage, rows, ostage, ret,
+               acc_out, meta_out, rhid, rg, ru, rd, stage, rows, ostage, ret,
                big, vg, vu, vd, acc, hbuf, obuf, gbuf, rbuf, ohbuf, meta, srow, rids,
                lsem, wl_sem, tok_sem, out_sem, ids_sem, hid_sem, w_ssem, w_rsem,
                row_ssem, row_rsem, ret_ssem, ret_rsem):
@@ -63,7 +80,8 @@
     load.wait()
     tt = min(256, tok)
     router = jnp.concatenate([wr[...], jnp.zeros((128 - ne, dm), BF16)], axis=0)
-    gain_f = gain[...].astype(F32)
+    gain_8 = gain[...].astype(F32)
+    gain_f = jnp.concatenate([gain_8[k:k + 1, :] for k in range(gain_8.shape[0])], axis=1)
 
     def normed_tile(rows_at):
         x = big[rows_at, :].astype(F32)
@@ -166,37 +184,24 @@
 
     tc = min(512, tok)
 
-    def out_copy(t):
-        at = pl.ds(pl.multiple_of(t * tc, tc), tc)
-        return pltpu.make_async_copy(big.at[at], out.at[at], out_sem.at[t])
-
-    def combine(fo, jo, i, last=False):
-        e = (jo * nf + fo) * per + i
+    def arrival(side, d, i):
+        return (side * nj + d) * per + i
+
+    def combine(side, d, i):
+        fo, jo = jnp.where(side == 1, of, f), lax.rem(j + nj - d, nj)
+        r = arrival(side, d, i)
 
         @pl.when(fo * nj + jo != me)
         def _():
-            pltpu.make_async_copy(ret.at[e], ret.at[e], ret_rsem.at[e]).wait()
-        fetch = pltpu.make_async_copy(ret.at[e], rbuf, lsem)
+            pltpu.make_async_copy(ret.at[r], ret.at[r], ret_rsem.at[r]).wait()
+        fetch = pltpu.make_async_copy(ret.at[r], rbuf, lsem)
         fetch.start()
         fetch.wait()
 
         @pl.loop(0, tok // tc)
         def _(t):
             at = pl.ds(pl.multiple_of(t * tc, tc), tc)
-            base = (e * cap).astype(F32)
-            m = meta[at, :]
-            s0, s1 = m[:, 0:1] - base, m[:, 1:2] - base
-            in0 = (s0 >= 0) & (s0 < cap)
-            in1 = (s1 >= 0) & (s1 < cap)
-            gate = jnp.where(in0, m[:, 2:3], jnp.where(in1, m[:, 3:4], 0.0))
-            lane = iota((tc, cap), 1)
-            hot = jnp.where((lane == s0.astype(jnp.int32)) | (lane == s1.astype(jnp.int32)), 1.0, 0.0).astype(BF16)
-            total = acc[at, :] + gate * jnp.dot(hot, rbuf[...], preferred_element_type=F32)
-            if last:
-                big[at, :] = total.astype(BF16)
-                out_copy(t).start()
-            else:
-                acc[at, :] = total
+            acc[at, :] = add_expert(acc[at, :], meta[at, :], rbuf[...], (jo * nf + fo) * per + i, cap)
 
     pair = 2 * cap
 
@@ -255,14 +260,15 @@
                 at = pl.ds(pl.multiple_of(t * tn, tn), tn)
                 obuf[:, at] = jnp.dot(hbuf[...], vd[:, at], preferred_element_type=F32).astype(BF16)
 
-            e = (j * nf + f) * per + i
             for q in range(2):
-                s = source(2 * p + q)
+                n = 2 * p + q
+                s = source(n)
+                r = arrival(jnp.where(n < nj, 1, 0), lax.rem(n, nj), i)
                 part = obuf.at[pl.ds(q * cap, cap)]
 
                 @pl.when(s == me)
                 def _():
-                    copy = pltpu.make_async_copy(part, ret.at[e], lsem)
+                    copy = pltpu.make_async_copy(part, ret.at[r], lsem)
                     copy.start()
                     copy.wait()
 
@@ -273,22 +279,24 @@
                     copy.start()
                     copy.wait()
                     pltpu.make_async_remote_copy(
-                        src_ref=ostage.at[k], dst_ref=ret.at[e], send_sem=ret_ssem.at[k],
-                        recv_sem=ret_rsem.at[e],
+                        src_ref=ostage.at[k], dst_ref=ret.at[r], send_sem=ret_ssem.at[k],
+                        recv_sem=ret_rsem.at[r],
                         device_id={'fsdp': s // nj, 'ep': lax.rem(s, nj)}, device_id_type=MESH).start()
 
         @pl.loop(0, nj)
         def _(d):
-            combine(f, lax.rem(j + nj - d, nj), i)
+            combine(0, d, i)
+
+    meta_copy = pltpu.make_async_copy(meta, meta_out, out_sem.at[1])
+    meta_copy.start()
 
     @pl.loop(0, nj * per - 1)
     def _(n):
-        combine(of, lax.rem(j + nj - lax.rem(n, nj), nj), n // nj)
-    combine(of, lax.rem(j + 1, nj), per - 1, last=True)
-
-    @pl.loop(0, tok // tc)
-    def _(t):
-        out_copy(t).wait()
+        combine(1, lax.rem(n, nj), n // nj)
+    acc_copy = pltpu.make_async_copy(acc, acc_out, out_sem.at[0])
+    acc_copy.start()
+    meta_copy.wait()
+    acc_copy.wait()
 
     @pl.loop(0, per)
     def _(i):
@@ -306,6 +314,9 @@
         @pl.when(lax.rem(k, ndev) != me)
         def _():
             pltpu.make_async_copy(ostage.at[k], ostage.at[k], ret_ssem.at[k]).wait()
+
+
+    pltpu.make_async_copy(ret.at[ne - 1], ret.at[ne - 1], ret_rsem.at[ne - 1]).wait()
 
 
 def local_block(nf, nj, hidden, norm_gain, w_router, w_gate, w_up, w_down, top2_ids):
@@ -321,7 +332,7 @@
     anyspec = pl.BlockSpec(memory_space=pl.ANY)
     vspec = pl.BlockSpec(memory_space=pltpu.VMEM)
     outs = [
-        sds((tok, dm), BF16), sds((tok, dm), BF16),
+        sds((tok, dm), F32), sds((tok, 128), F32), sds((tok, dm), BF16),
         sds((per, half, ff), BF16), sds((per, half, ff), BF16), sds((per, ff, half), BF16),
         sds((2 * nj * per, cap, dm), BF16), sds((per, ndev * cap, dm), BF16),
         sds((per * ndev, cap, dm), BF16), sds((ne, cap, dm), BF16),
@@ -334,11 +345,11 @@
         pltpu.VMEM((2 * cap, ff), BF16), pltpu.VMEM((2 * cap, dm), BF16),
         pltpu.VMEM((cap, dm), BF16), pltpu.VMEM((cap, dm), BF16), pltpu.VMEM((cap, tok), BF16),
         pltpu.VMEM((tok, 128), F32), pltpu.VMEM((8, tok), F32), pltpu.VMEM((2, tok), jnp.int32),
-        dma, dma((6,)), dma((ndev,)), dma((8,)), dma((2,)), dma((2,)), dma((3 * per,)), dma((3 * per,)),
+        dma, dma((6,)), dma((ndev,)), dma((2,)), dma((2,)), dma((2,)), dma((3 * per,)), dma((3 * per,)),
         dma((2 * nj * per,)), dma((per * ndev,)), dma((per * ndev,)), dma((ne,)),
     ]
     flops = 6 * per * ndev * cap * dm * ff + 3 * 2 * ne * cap * tok * dm
-    result = pl.pallas_call(
+    acc, meta, *_, ret = pl.pallas_call(
         functools.partial(moe_kernel, cfg),
         out_shape=outs,
         in_specs=[anyspec, vspec, vspec, anyspec, anyspec, anyspec, vspec],
@@ -347,8 +358,18 @@
         compiler_params=pltpu.CompilerParams(collective_id=0, has_side_effects=True, vmem_limit_bytes=67043328),
         cost_estimate=pl.CostEstimate(flops=flops, bytes_accessed=400 * 1024 * 1024, transcendentals=0),
         name='moe_block',
-    )(hidden, norm_gain.reshape(1, dm), w_router.T, w_gate, w_up, w_down, top2_ids.T)
-    return result[0]
+    )(hidden, norm_gain.reshape(dm // 128, 128), w_router.T, w_gate, w_up, w_down, top2_ids.T)
+    tc = min(512, tok)
+    return pl.pallas_call(
+        functools.partial(last_kernel, nf, nj, per, cap),
+        out_shape=sds((tok, dm), BF16),
+        grid=(tok // tc,),
+        in_specs=[pl.BlockSpec((tc, dm), lambda t: (t, 0)), pl.BlockSpec((tc, 128), lambda t: (t, 0)),
+                  pl.BlockSpec((1, cap, dm), lambda t: (ne - 1, 0, 0))],
+        out_specs=pl.BlockSpec((tc, dm), lambda t: (t, 0)),
+        cost_estimate=pl.CostEstimate(flops=2 * tok * cap * dm, bytes_accessed=26 * 1024 * 1024, transcendentals=0),
+        name='moe_last',
+    )(acc, meta, ret)
 
 
 def solution(mesh):

time: 1250 us -> 1250 us (level)
  Pallas kernels: 1230 us -> 1250 us
    pallas_call x0 -> x1, Pallas kernels: none -> 14.1 us  [local_block(): pl.pallas_call(functools.partial(last_kernel, nf, nj, per, cap), out_shap...]
where the time goes in v3:
time: 1250 us
  Pallas kernels  1250 us (100%)
    pallas_call x1, Pallas kernels, local_block(): pl.pallas_call(functools.partial(moe_kernel, cfg), out_shape=outs, in_spe...  1230 us

profile of v3, /device:TPU:0, one launch (start us, length us, event | category | flops | bytes accessed | tf_op | source)
XLA Modules:
  0.0 1247.0 jit_solution(5872305828194618354)
XLA Ops:
  0.0 1233.0 %moe_block.1 = (f32[4096,1024]{1,0:T(8,128)}, f32[4096,128]{1,0:T(8,128)}, bf16[4096,1024]{1,0:T(8,128)(2,1)}, bf16[4,512,2816]{2,1,0:T(8,128)(2,1)}, bf16[4,512...) custom-call(bf16[4096,1024]{1,0:T(8,128)(2,1)} %hid.1, ...), custom_call_target="tpu_custom_call" | custom-call | flops 434865438720 | bytes 419430400 | tf_op jit(solution)/shard_map/moe_block/pallas_call | solution.py:352
  1233.0 14.1 %moe_last.1 = bf16[4096,1024]{1,0:T(8,128)(2,1)} custom-call(f32[4096,1024]{1,0:T(8,128)} %get-tuple-element.8.acc, f32[4096,128]{1,0:T(8,128)} %get-tuple-element.9.meta, bf16[32,320,1024]{2,1,0:T(8,128)(2,1)} %get-tuple-element.10.ret), custom_call_target="tpu_custom_call" | custom-call | flops 2684354560 | bytes 27262976 | tf_op jit(solution)/shard_map/moe_last/pallas_call | solution.py:363
